TPU v7x, 256 devices: a whole 4x4x8 slice. The times are simulated.
256 devices in a mesh: gx: 4 (over x), gy: 8 (over y, core), gz: 8 (over z).
Axes of the slice: x: 4, y: 4, z: 8, core: 2. Of those that a mesh axis runs over, the one named last changes fastest.
Arguments:
- ham_blocks: bfloat16 [2048, 128, 128], P(('gx', 'gy', 'gz')), may hold values from -0.119628906 to 0.119628906
- onsite: float32 [256, 768], P(('gx', 'gy', 'gz')), may hold values from -1 to 1
- entry_slot: int32 [256, 36], P(('gx', 'gy', 'gz')), may hold values from 0 to 63, as said below
- send_table: int32 [256, 64, 1], P(('gx', 'gy', 'gz')), may hold values from -1 to 7, as said below
- reads: int32 [256, 8], P(('gx', 'gy', 'gz')), may hold values from 0 to 42, as said below
- gram_targets: int32 [256, 7, 8], P(('gx', 'gy', 'gz')), may hold values from 0 to 36, as said below
- table_pick: int32 [256, 2, 8], P(('gx', 'gy', 'gz')), may hold values from 0 to 3, as said below
- phi: bfloat16 [256, 4, 128, 4096], P(('gx', 'gy', 'gz')), may hold values from -2.390625 to 2.390625
- potential_in: float32 [16, 64, 1024], P('gx', 'gy', 'gz'), may hold values from -1.5 to 1.5
Outputs:
- potential: float32 [16, 64, 1024], P('gx', 'gy', 'gz')
- grid_blocks: float32 [2048, 128, 128], P(('gx', 'gy', 'gz'))
Inputs may be any that keep to these rules, and one draw needn't show every extreme that they name: `entry_slot`: row d holds distinct slot numbers; at most 1 entries of one submatrix come from one device of its plane, and some device gives exactly 1. send_table[o, e, c] is the local block that submatrix e of o's plane reads in slot o's plane number + c, and -1 where e reads no block in that slot. `reads`: 42 marks an unused slot; some brick uses all 8 slots; the number of used slots differs widely between bricks. gram_targets[d, k, r] is 36 where slot r of the brick at face k of d is unused, and an entry below 36 where it is used; one entry of a submatrix receives at most two slots. `table_pick`: the two tables of one slot differ.
All inputs are finite; a program needn't handle non-finite values.
Results may differ from a plain program's by a relative error of at most 0.012.
Values may be sent and summed in bfloat16 or wider, within the bound.
No kernel may reach another device: no remote copies, remote signals or barrier semaphores. Data moves between devices by JAX's collectives and lax.ppermute only.
A program may use at most 128 MiB of HBM per device.

v0:
```python
import jax
import jax.numpy as jnp
from jax import lax
from jax.sharding import PartitionSpec as P

B = 128
S = 6
M = 768


EPSILON = 1e-06


def extended_2(x, sides, width):
    edges = {}
    for axis, dim in sides:
        size, length = (lax.axis_size(axis), x.shape[dim])
        up = [(i, (i + 1) % size) for i in range(size)]
        last = lax.slice_in_dim(x, length - width, length, axis=dim)
        first = lax.slice_in_dim(x, 0, width, axis=dim)
        edges[dim] = (
            lax.ppermute(last, axis, up),
            lax.ppermute(first, axis, [(b, a) for a, b in up]),
        )
    done = []
    for _, dim in sides:
        low, high = edges[dim]
        around = [(width, width) if d in done else (0, 0) for d in range(x.ndim)]
        x = jnp.concatenate([jnp.pad(low, around), x, jnp.pad(high, around)], axis=dim)
        done.append(dim)
    return x


def density_columns(matrix, onsite_row):
    wide = matrix.astype(jnp.float32)
    hamilton = 0.5 * (wide + wide.T) + jnp.diag(onsite_row)
    factor = lax.rsqrt(jnp.sum(hamilton * hamilton) / M + EPSILON) / 1.3
    start = (hamilton * factor).astype(jnp.bfloat16)
    square = jnp.dot(start, start, preferred_element_type=jnp.float32).astype(jnp.bfloat16)
    cube = jnp.dot(start, square, preferred_element_type=jnp.float32)
    first = (1.5 * start.astype(jnp.float32) - 0.5 * cube).astype(jnp.bfloat16)
    column = first[:, :B]
    inner = jnp.dot(first, column, preferred_element_type=jnp.float32).astype(jnp.bfloat16)
    outer = jnp.dot(first, inner, preferred_element_type=jnp.float32)
    unit = (jnp.arange(M)[:, None] == jnp.arange(B)[None, :]).astype(jnp.float32)
    result = 0.5 * (unit - (1.5 * column.astype(jnp.float32) - 0.5 * outer))
    return result.astype(jnp.bfloat16).reshape(S, B, B)


def face_stack(extended):
    return jnp.stack(
        [
            extended[1, 1, 1],
            extended[0, 1, 1],
            extended[2, 1, 1],
            extended[1, 0, 1],
            extended[1, 2, 1],
            extended[1, 1, 0],
            extended[1, 1, 2],
        ]
    )


def jacobi_step(padded, source):
    beside_all = padded[2:, 1:-1, 1:-1] + padded[:-2, 1:-1, 1:-1]
    beside_all = beside_all + padded[1:-1, 2:, 1:-1] + padded[1:-1, :-2, 1:-1]
    beside_all = beside_all + padded[1:-1, 1:-1, 2:] + padded[1:-1, 1:-1, :-2]
    return (beside_all + source) / 6.0


def shards(
    ham_blocks, onsite, entry_slot, send_table, reads, gram_targets, table_pick, phi, potential_in
):
    plane = lax.axis_size(("gy", "gz"))
    held = ham_blocks.shape[0]
    lanes_count = send_table.shape[2]
    slot_ids = entry_slot[0]
    picks = send_table[0]
    fetched = jnp.take(ham_blocks, jnp.maximum(picks, 0), axis=0)
    outgoing = jnp.where((picks >= 0)[:, :, None, None], fetched, jnp.zeros((), jnp.bfloat16))
    incoming = lax.all_to_all(outgoing, ("gy", "gz"), split_axis=0, concat_axis=0, tiled=True)
    entries = jnp.take(incoming.reshape(plane * lanes_count, B, B), slot_ids, axis=0)
    matrix = entries.reshape(S, S, B, B).transpose(0, 2, 1, 3).reshape(M, M)
    density = density_columns(matrix, onsite[0])
    density_ext = extended_2(density[None, None, None], (("gx", 0), ("gy", 1), ("gz", 2)), 1)
    candidates = jnp.concatenate(
        [face_stack(density_ext).reshape(7 * S, B, B), jnp.zeros((1, B, B), jnp.bfloat16)]
    )
    chosen_blocks = jnp.take(candidates, reads[0], axis=0)
    left_table = jnp.take(phi[0], table_pick[0, 0], axis=0)
    right_table = jnp.take(phi[0], table_pick[0, 1], axis=0)
    mixed = jnp.einsum(
        "rij,rig->rjg", chosen_blocks, left_table, preferred_element_type=jnp.float32
    )
    source = jnp.sum(mixed * right_table, axis=(0, 1)).reshape(potential_in.shape)
    potential = potential_in
    for sweep_index in range(2):
        padded = extended_2(potential, (("gx", 0), ("gy", 1), ("gz", 2)), 1)
        potential = jacobi_step(padded, source)
    weighted = (right_table * potential.reshape(-1)[None, None, :]).astype(jnp.bfloat16)
    grams = jnp.einsum(
        "rig,rjg->rij", left_table, weighted, preferred_element_type=jnp.float32
    ).astype(jnp.bfloat16)
    gram_ext = extended_2(grams[None, None, None], (("gx", 0), ("gy", 1), ("gz", 2)), 1)
    gathered = face_stack(gram_ext).reshape(7 * grams.shape[0], B, B)
    selector = (gram_targets[0].reshape(-1)[None, :] == jnp.arange(S * S)[:, None]).astype(
        jnp.bfloat16
    )
    summed = jnp.einsum(
        "sq,qij->sij", selector, gathered, preferred_element_type=jnp.float32
    ).astype(jnp.bfloat16)
    placement = (jnp.arange(plane * lanes_count)[:, None] == slot_ids[None, :]).astype(jnp.bfloat16)
    outgoing_back = jnp.einsum("qs,sij->qij", placement, summed, preferred_element_type=jnp.float32)
    outgoing_back = outgoing_back.astype(jnp.bfloat16).reshape(plane, lanes_count, B, B)
    arrived = lax.all_to_all(
        outgoing_back, ("gy", "gz"), split_axis=0, concat_axis=0, tiled=True
    ).reshape(plane * lanes_count, B, B)
    owner_select = (send_table[0].reshape(-1)[None, :] == jnp.arange(held)[:, None]).astype(
        jnp.bfloat16
    )
    grid_blocks = jnp.einsum(
        "hq,qij->hij", owner_select, arrived, preferred_element_type=jnp.float32
    )
    return (potential, grid_blocks)


def solution(mesh):
    placed = (
        P(("gx", "gy", "gz"), None, None),
        P(("gx", "gy", "gz"), None),
        P(("gx", "gy", "gz"), None),
        P(("gx", "gy", "gz"), None, None),
        P(("gx", "gy", "gz"), None),
        P(("gx", "gy", "gz"), None, None),
        P(("gx", "gy", "gz"), None, None),
        P(("gx", "gy", "gz"), None, None, None),
        P("gx", "gy", "gz"),
    )
    return jax.shard_map(
        shards,
        mesh=mesh,
        in_specs=placed,
        out_specs=(P("gx", "gy", "gz"), P(("gx", "gy", "gz"), None, None)),
        check_vma=False,
    )
```

profile of v0, /device:TPU:1, one launch (start us, length us, event | category | flops | bytes accessed | tf_op | source)
XLA Modules:
  0.0 224.1 jit_solution(11811517555407620996)
XLA Ops:
  5.3 13.3 %all-to-all-start = ((bf16[64,1,128,128]{3,2,1,0:T(8,128)(2,1)}), bf16[64,1,128,128]{3,2,1,0:T(8,128)(2,1)S(1)}, u32[]{:S(2)}, u32[]{:S(2)}) async-start(bf16[64,1,128,128]{3,2,1,0:T(8,128)(2,1)} %fusion.9), calls=%async_computation | async-start | bytes 4194304 | tf_op jit(solution)/shard_map/all_to_all | solution.py:81
  21.5 2.6 %collective-permute-start.4 = (f32[4,8,1]{2,1,0:T(8,128)S(1)}, f32[4,8,1]{2,1,0:T(8,128)S(1)}, u32[]{:S(2)}, u32[]{:S(2)}) collective-permute-start(f32[4,8,1]{2,1,0:T(8,128)S(1)} %get-tuple-element.19), channel_id=1, source_target_pairs={{1,0},{2,1},{3,2},{4,3},{5,4},{6,5},{7,6},{0,7},{9,8},{10,9},{11,1... | collective-permute-start | bytes 392 | tf_op jit(solution)/shard_map/ppermute | solution.py:23
  28.7 6.8 %gather_fusion.3 = bf16[8,128,4096]{2,1,0:T(8,128)(2,1)} fusion(bf16[4,128,4096]{2,1,0:T(8,128)(2,1)} %bitcast.109, s32[1024]{0:T(1024)S(1)} %get-tuple-element.32), kind=kCustom, calls=%fused_computation.clone | custom fusion | bytes 16777248 | tf_op jit(solution)/shard_map/jit(_take)/gather | solution.py:90
  35.6 6.8 %gather_fusion.4 = bf16[8,128,4096]{2,1,0:T(8,128)(2,1)} fusion(bf16[4,128,4096]{2,1,0:T(8,128)(2,1)} %bitcast.110, s32[1024]{0:T(1024)S(1)} %get-tuple-element.31), kind=kCustom, calls=%fused_computation.1.clone | custom fusion | bytes 16777248 | tf_op jit(solution)/shard_map/jit(_take)/gather | solution.py:91
  42.7 28.0 %all-to-all-done = bf16[64,1,128,128]{3,2,1,0:T(8,128)(2,1)S(1)} async-done(((bf16[64,1,128,128]{3,2,1,0:T(8,128)(2,1)}), bf16[64,1,128,128]{3,2,1,0:T(8,128)(2,1)S(1)}, u32[]{:S(2)}, u32[]{:S(2)}) %all-to-all-start) | async-done | bytes 2097184 | tf_op jit(solution)/shard_map/all_to_all | solution.py:81
  72.6 2.1 fusion.16
  76.6 3.1 %copy.20 = f32[768,768]{0,1:T(8,128)} copy(f32[768,768]{1,0:T(8,128)} %bitcast.113) | data formatting | bytes 4718592 | tf_op jit(solution)/shard_map/convert_element_type | solution.py:35
  79.7 3.1 %multiply_reduce_fusion = f32[]{:T(128)} fusion(f32[768]{0:T(1024)S(1)} %reduce.1, f32[768,768]{0,1:T(8,128)} %copy.20, f32[96,8,6,128]{3,2,1,0:T(8,128)S(1)} %bitcast.112), kind=kLoop, calls=%fused_computation.19 | loop fusion | flops 4128767 | bytes 4721668 | tf_op jit(solution)/shard_map/reduce_sum | solution.py:37
  83.4 9.0 %subtract_convert_fusion = bf16[768,768]{1,0:T(8,128)(2,1)S(1)} fusion(f32[]{:T(128)S(6)} %div.13, f32[768]{0:T(1024)S(1)} %reduce.1, f32[768,768]{1,0:T(8,128)} %bitcast.114, f32[768,768]{0,1:T(8,128)} %copy.20), kind=kOutput, calls=%fused_computation.17 | convolution fusion | flops 1827864576 | bytes 5901316 | tf_op jit(solution)/shard_map/dot_general | solution.py:40
  96.8 4.2 %collective-permute-done.6 = bf16[1,1,1,6,128,128]{5,4,3,2,1,0:T(8,128)(2,1)S(1)} collective-permute-done((bf16[1,1,1,6,128,128]{5,4,3,2,1,0:T(8,128)(2,1)S(1)}, bf16[1,1,1,6,128,128]{5,4,3,2,1,0:T(8,128)(2,1)S(1)}, u32[]{:S(2)}, u32[]{:S(2)}) %collective-permute-start.6) | collective-permute-done | bytes 196640 | tf_op jit(solution)/shard_map/ppermute | solution.py:22
  102.1 2.2 collective-permute-start.11
  104.3 2.0 collective-permute-done.9
  109.0 9.4 %fusion = f32[4096]{0:T(1024)S(1)} fusion(bf16[8,128,4096]{2,1,0:T(8,128)(2,1)} %gather_fusion.3, pred[8]{0:T(512)(128)(4,1)S(1)} %copy-done.7, bf16[8,128,4096]{2,1,0:T(8,128)(2,1)} %gather_fusion.4, pred[8]{0:T(512)(128)(4,1)S(1)} %get-tuple-element.9, bf16[8,128,128]{2,1,0:T(8,128)(2,1)S(1)} %gather_fusion.2, pred[8]{0:T(512)(128)(4,1)S(1)} %copy-done.10), kind=kOutput, calls=%fused_computation.7 | convolution fusion | flops 1094840320 | bytes 17055768 | tf_op jit(solution)/shard_map/rij,rig->rjg/dot_general | solution.py:92
  118.5 2.8 %collective-permute-start.12 = (f32[1,8,128]{2,1,0:T(8,128)S(1)}, f32[1,8,128]{2,1,0:T(8,128)S(1)}, u32[]{:S(2)}, u32[]{:S(2)}) collective-permute-start(f32[1,8,128]{2,1,0:T(8,128)S(1)} %get-tuple-element.16), channel_id=1, source_target_pairs={{64,0},{128,64},{192,128},{0,192},{65,1},{129,65},{193,129},{1,193... | collective-permute-start | bytes 12296 | tf_op jit(solution)/shard_map/ppermute | solution.py:23
  123.2 2.8 %collective-permute-start.16 = (f32[4,8,1]{2,1,0:T(8,128)S(1)}, f32[4,8,1]{2,1,0:T(8,128)S(1)}, u32[]{:S(2)}, u32[]{:S(2)}) collective-permute-start(f32[4,8,1]{2,1,0:T(8,128)S(1)} %get-tuple-element.13), channel_id=1, source_target_pairs={{1,0},{2,1},{3,2},{4,3},{5,4},{6,5},{7,6},{0,7},{9,8},{10,9},{11,1... | collective-permute-start | bytes 392 | tf_op jit(solution)/shard_map/ppermute | solution.py:23
  126.9 2.9 %collective-permute-done.17 = f32[4,8,1]{2,1,0:T(8,128)S(1)} collective-permute-done((f32[4,8,1]{2,1,0:T(8,128)S(1)}, f32[4,8,1]{2,1,0:T(8,128)S(1)}, u32[]{:S(2)}, u32[]{:S(2)}) %collective-permute-start.17) | collective-permute-done | bytes 160 | tf_op jit(solution)/shard_map/ppermute | solution.py:22
  129.9 8.4 %bitcast_dynamic-update-slice_fusion.6 = (bf16[7,8,128,128]{3,2,1,0:T(8,128)(2,1)S(1)}, bf16[8,128,128]{2,1,0:T(8,128)(2,1)S(1)}) fusion(f32[4096]{0:T(1024)S(1)} %fusion.74, bf16[8,128,4096]{2,1,0:T(8,128)(2,1)} %gather_fusion.4, pred[8]{0:T(512)(128)(4,1)S(1)} %get-tuple-element.9, bf16[8,128,4096]{2,1,0:T(8,128)(2,1)} %gather_fusion.3, ...), kind=kOutput, calls=%fused_computation.47 | convolution fusion | flops 1094844416 | bytes 17317904 | tf_op jit(solution)/shard_map/rig,rjg->rij/dot_general | solution.py:101
  138.8 2.8 %collective-permute-start.19 = (bf16[1,1,1,8,128,128]{5,4,3,2,1,0:T(8,128)(2,1)S(1)}, bf16[1,1,1,8,128,128]{5,4,3,2,1,0:T(8,128)(2,1)S(1)}, u32[]{:S(2)}, u32[]{:S(2)}) collective-permute-start(bf16[1,1,1,8,128,128]{5,4,3,2,1,0:T(8,128)(2,1)S(1)} %bitcast.129), channel_id=1, source_target_pairs={{64,0},{128,64},{192,128},{0,192},{65,1},{129,65},{193,129},{1,193... | collective-permute-start | bytes 786440 | tf_op jit(solution)/shard_map/ppermute | solution.py:23
  143.8 2.4 %collective-permute-done.18 = bf16[1,1,1,8,128,128]{5,4,3,2,1,0:T(8,128)(2,1)S(1)} collective-permute-done((bf16[1,1,1,8,128,128]{5,4,3,2,1,0:T(8,128)(2,1)S(1)}, bf16[1,1,1,8,128,128]{5,4,3,2,1,0:T(8,128)(2,1)S(1)}, u32[]{:S(2)}, u32[]{:S(2)}) %collective-permute-start.18) | collective-permute-done | bytes 262176 | tf_op jit(solution)/shard_map/ppermute | solution.py:22
  146.7 2.7 %collective-permute-done.21 = bf16[1,1,1,8,128,128]{5,4,3,2,1,0:T(8,128)(2,1)S(1)} collective-permute-done((bf16[1,1,1,8,128,128]{5,4,3,2,1,0:T(8,128)(2,1)S(1)}, bf16[1,1,1,8,128,128]{5,4,3,2,1,0:T(8,128)(2,1)S(1)}, u32[]{:S(2)}, u32[]{:S(2)}) %collective-permute-start.21) | collective-permute-done | bytes 262176 | tf_op jit(solution)/shard_map/ppermute | solution.py:23
  153.0 3.6 %convert_bitcast_fusion = bf16[64,1,128,128]{3,0,2,1:T(8,128)(2,1)S(1)} fusion(bf16[56,128,128]{2,1,0:T(8,128)(2,1)} %bitcast.117, s32[56]{0:T(128)S(1)} %eq.68, s32[36]{0:T(128)S(1)} %bitcast.126), kind=kOutput, calls=%fused_computation.26 | convolution fusion | flops 143200480 | bytes 3932528 | tf_op jit(solution)/shard_map/qs,sij->qij/dot_general | solution.py:113
  156.7 2.7 %copy.23 = bf16[64,1,128,128]{3,2,1,0:T(8,128)(2,1)} copy(bf16[64,1,128,128]{3,0,2,1:T(8,128)(2,1)S(1)} %convert_bitcast_fusion) | data formatting | bytes 4194304 | tf_op jit(solution)/shard_map/reshape | solution.py:114
  159.4 10.8 %all-to-all-start.1 = ((bf16[64,1,128,128]{3,2,1,0:T(8,128)(2,1)}), bf16[64,1,128,128]{3,2,1,0:T(8,128)(2,1)S(1)}, u32[]{:S(2)}, u32[]{:S(2)}) async-start(bf16[64,1,128,128]{3,2,1,0:T(8,128)(2,1)} %copy.23), calls=%async_computation.1 | async-start | bytes 4194304 | tf_op jit(solution)/shard_map/all_to_all | solution.py:115
  170.9 51.1 %all-to-all-done.1 = bf16[64,1,128,128]{3,2,1,0:T(8,128)(2,1)S(1)} async-done(((bf16[64,1,128,128]{3,2,1,0:T(8,128)(2,1)}), bf16[64,1,128,128]{3,2,1,0:T(8,128)(2,1)S(1)}, u32[]{:S(2)}, u32[]{:S(2)}) %all-to-all-start.1) | async-done | bytes 2097184 | tf_op jit(solution)/shard_map/all_to_all | solution.py:115
  (114 shorter events, 36.9 us)
Async XLA Ops:
  5.3 65.4 %all-to-all-start = ((bf16[64,1,128,128]{3,2,1,0:T(8,128)(2,1)}), bf16[64,1,128,128]{3,2,1,0:T(8,128)(2,1)S(1)}, u32[]{:S(2)}, u32[]{:S(2)}) async-start(bf16[64,1,128,128]{3,2,1,0:T(8,128)(2,1)} %fusion.9), calls=%async_computation | async-start | bytes 4194304 | tf_op jit(solution)/shard_map/all_to_all | solution.py:81
  18.6 24.0 %collective-permute-start.1 = (f32[1,8,128]{2,1,0:T(8,128)S(1)}, f32[1,8,128]{2,1,0:T(8,128)S(1)}, u32[]{:S(2)}, u32[]{:S(2)}) collective-permute-start(f32[1,8,128]{2,1,0:T(8,128)S(1)} %get-tuple-element.24), channel_id=1, source_target_pairs={{0,64},{64,128},{128,192},{192,0},{1,65},{65,129},{129,193},{193,1... | collective-permute-start | bytes 12296 | tf_op jit(solution)/shard_map/ppermute | solution.py:22
  19.9 75.1 %collective-permute-start = (f32[1,8,128]{2,1,0:T(8,128)S(1)}, f32[1,8,128]{2,1,0:T(8,128)S(1)}, u32[]{:S(2)}, u32[]{:S(2)}) collective-permute-start(f32[1,8,128]{2,1,0:T(8,128)S(1)} %get-tuple-element.23), channel_id=1, source_target_pairs={{64,0},{128,64},{192,128},{0,192},{65,1},{129,65},{193,129},{1,193... | collective-permute-start | bytes 12296 | tf_op jit(solution)/shard_map/ppermute | solution.py:23
  21.5 96.9 %collective-permute-start.4 = (f32[4,8,1]{2,1,0:T(8,128)S(1)}, f32[4,8,1]{2,1,0:T(8,128)S(1)}, u32[]{:S(2)}, u32[]{:S(2)}) collective-permute-start(f32[4,8,1]{2,1,0:T(8,128)S(1)} %get-tuple-element.19), channel_id=1, source_target_pairs={{1,0},{2,1},{3,2},{4,3},{5,4},{6,5},{7,6},{0,7},{9,8},{10,9},{11,1... | collective-permute-start | bytes 392 | tf_op jit(solution)/shard_map/ppermute | solution.py:23
  24.0 18.3 %collective-permute-start.2 = (f32[4,1,128]{2,1,0:T(1,128)S(1)}, f32[4,1,128]{2,1,0:T(1,128)S(1)}, u32[]{:S(2)}, u32[]{:S(2)}) collective-permute-start(f32[4,1,128]{2,1,0:T(1,128)S(1)} %get-tuple-element.22), channel_id=1, source_target_pairs={{8,0},{16,8},{24,16},{32,24},{40,32},{48,40},{56,48},{0,56},{9,1},... | collective-permute-start | bytes 6152 | tf_op jit(solution)/shard_map/ppermute | solution.py:23
  25.3 17.4 %collective-permute-start.3 = (f32[4,1,128]{2,1,0:T(1,128)S(1)}, f32[4,1,128]{2,1,0:T(1,128)S(1)}, u32[]{:S(2)}, u32[]{:S(2)}) collective-permute-start(f32[4,1,128]{2,1,0:T(1,128)S(1)} %get-tuple-element.21), channel_id=1, source_target_pairs={{0,8},{8,16},{16,24},{24,32},{32,40},{40,48},{48,56},{56,0},{1,9},... | collective-permute-start | bytes 6152 | tf_op jit(solution)/shard_map/ppermute | solution.py:22
  42.4 76.0 %collective-permute-start.5 = (f32[4,8,1]{2,1,0:T(8,128)S(1)}, f32[4,8,1]{2,1,0:T(8,128)S(1)}, u32[]{:S(2)}, u32[]{:S(2)}) collective-permute-start(f32[4,8,1]{2,1,0:T(8,128)S(1)} %get-tuple-element.20), channel_id=1, source_target_pairs={{0,1},{1,2},{2,3},{3,4},{4,5},{5,6},{6,7},{7,0},{8,9},{9,10},{10,1... | collective-permute-start | bytes 392 | tf_op jit(solution)/shard_map/ppermute | solution.py:22
  93.8 7.2 %collective-permute-start.6 = (bf16[1,1,1,6,128,128]{5,4,3,2,1,0:T(8,128)(2,1)S(1)}, bf16[1,1,1,6,128,128]{5,4,3,2,1,0:T(8,128)(2,1)S(1)}, u32[]{:S(2)}, u32[]{:S(2)}) collective-permute-start(bf16[1,1,1,6,128,128]{5,4,3,2,1,0:T(8,128)(2,1)S(1)} %bitcast.119), channel_id=1, source_target_pairs={{0,64},{64,128},{128,192},{192,0},{1,65},{65,129},{129,193},{193,1... | collective-permute-start | bytes 589832 | tf_op jit(solution)/shard_map/ppermute | solution.py:22
  95.1 6.2 %collective-permute-start.7 = (bf16[1,1,1,6,128,128]{5,4,3,2,1,0:T(8,128)(2,1)S(1)}, bf16[1,1,1,6,128,128]{5,4,3,2,1,0:T(8,128)(2,1)S(1)}, u32[]{:S(2)}, u32[]{:S(2)}) collective-permute-start(bf16[1,1,1,6,128,128]{5,4,3,2,1,0:T(8,128)(2,1)S(1)} %bitcast.120), channel_id=1, source_target_pairs={{64,0},{128,64},{192,128},{0,192},{65,1},{129,65},{193,129},{1,193... | collective-permute-start | bytes 589832 | tf_op jit(solution)/shard_map/ppermute | solution.py:23
  96.5 5.6 %collective-permute-start.8 = (bf16[1,1,1,6,128,128]{5,4,3,2,1,0:T(8,128)(2,1)S(1)}, bf16[1,1,1,6,128,128]{5,4,3,2,1,0:T(8,128)(2,1)S(1)}, u32[]{:S(2)}, u32[]{:S(2)}) collective-permute-start(bf16[1,1,1,6,128,128]{5,4,3,2,1,0:T(8,128)(2,1)S(1)} %bitcast.121), channel_id=1, source_target_pairs={{0,8},{8,16},{16,24},{24,32},{32,40},{40,48},{48,56},{56,0},{1,9},... | collective-permute-start | bytes 589832 | tf_op jit(solution)/shard_map/ppermute | solution.py:22
  101.0 5.4 %collective-permute-start.9 = (bf16[1,1,1,6,128,128]{5,4,3,2,1,0:T(8,128)(2,1)S(1)}, bf16[1,1,1,6,128,128]{5,4,3,2,1,0:T(8,128)(2,1)S(1)}, u32[]{:S(2)}, u32[]{:S(2)}) collective-permute-start(bf16[1,1,1,6,128,128]{5,4,3,2,1,0:T(8,128)(2,1)S(1)} %bitcast.123), channel_id=1, source_target_pairs={{8,0},{16,8},{24,16},{32,24},{40,32},{48,40},{56,48},{0,56},{9,1},... | collective-permute-start | bytes 589832 | tf_op jit(solution)/shard_map/ppermute | solution.py:23
  101.3 6.1 %collective-permute-start.10 = (bf16[1,1,1,6,128,128]{5,4,3,2,1,0:T(8,128)(2,1)S(1)}, bf16[1,1,1,6,128,128]{5,4,3,2,1,0:T(8,128)(2,1)S(1)}, u32[]{:S(2)}, u32[]{:S(2)}) collective-permute-start(bf16[1,1,1,6,128,128]{5,4,3,2,1,0:T(8,128)(2,1)S(1)} %bitcast.124), channel_id=1, source_target_pairs={{0,1},{1,2},{2,3},{3,4},{4,5},{5,6},{6,7},{7,0},{8,9},{9,10},{10,1... | collective-permute-start | bytes 589832 | tf_op jit(solution)/shard_map/ppermute | solution.py:22
  102.1 6.0 %collective-permute-start.11 = (bf16[1,1,1,6,128,128]{5,4,3,2,1,0:T(8,128)(2,1)S(1)}, bf16[1,1,1,6,128,128]{5,4,3,2,1,0:T(8,128)(2,1)S(1)}, u32[]{:S(2)}, u32[]{:S(2)}) collective-permute-start(bf16[1,1,1,6,128,128]{5,4,3,2,1,0:T(8,128)(2,1)S(1)} %bitcast.125), channel_id=1, source_target_pairs={{1,0},{2,1},{3,2},{4,3},{5,4},{6,5},{7,6},{0,7},{9,8},{10,9},{11,1... | collective-permute-start | bytes 589832 | tf_op jit(solution)/shard_map/ppermute | solution.py:23
  118.5 11.3 %collective-permute-start.12 = (f32[1,8,128]{2,1,0:T(8,128)S(1)}, f32[1,8,128]{2,1,0:T(8,128)S(1)}, u32[]{:S(2)}, u32[]{:S(2)}) collective-permute-start(f32[1,8,128]{2,1,0:T(8,128)S(1)} %get-tuple-element.16), channel_id=1, source_target_pairs={{64,0},{128,64},{192,128},{0,192},{65,1},{129,65},{193,129},{1,193... | collective-permute-start | bytes 12296 | tf_op jit(solution)/shard_map/ppermute | solution.py:23
  121.3 8.5 %collective-permute-start.13 = (f32[1,8,128]{2,1,0:T(8,128)S(1)}, f32[1,8,128]{2,1,0:T(8,128)S(1)}, u32[]{:S(2)}, u32[]{:S(2)}) collective-permute-start(f32[1,8,128]{2,1,0:T(8,128)S(1)} %get-tuple-element.15), channel_id=1, source_target_pairs={{0,64},{64,128},{128,192},{192,0},{1,65},{65,129},{129,193},{193,1... | collective-permute-start | bytes 12296 | tf_op jit(solution)/shard_map/ppermute | solution.py:22
  121.3 4.7 %collective-permute-start.14 = (f32[4,1,128]{2,1,0:T(1,128)S(1)}, f32[4,1,128]{2,1,0:T(1,128)S(1)}, u32[]{:S(2)}, u32[]{:S(2)}) collective-permute-start(f32[4,1,128]{2,1,0:T(1,128)S(1)} %get-tuple-element.18), channel_id=1, source_target_pairs={{8,0},{16,8},{24,16},{32,24},{40,32},{48,40},{56,48},{0,56},{9,1},... | collective-permute-start | bytes 6152 | tf_op jit(solution)/shard_map/ppermute | solution.py:23
  126.0 3.8 %collective-permute-start.17 = (f32[4,8,1]{2,1,0:T(8,128)S(1)}, f32[4,8,1]{2,1,0:T(8,128)S(1)}, u32[]{:S(2)}, u32[]{:S(2)}) collective-permute-start(f32[4,8,1]{2,1,0:T(8,128)S(1)} %get-tuple-element.14), channel_id=1, source_target_pairs={{0,1},{1,2},{2,3},{3,4},{4,5},{5,6},{6,7},{7,0},{8,9},{9,10},{10,1... | collective-permute-start | bytes 392 | tf_op jit(solution)/shard_map/ppermute | solution.py:22
  138.4 7.8 %collective-permute-start.18 = (bf16[1,1,1,8,128,128]{5,4,3,2,1,0:T(8,128)(2,1)S(1)}, bf16[1,1,1,8,128,128]{5,4,3,2,1,0:T(8,128)(2,1)S(1)}, u32[]{:S(2)}, u32[]{:S(2)}) collective-permute-start(bf16[1,1,1,8,128,128]{5,4,3,2,1,0:T(8,128)(2,1)S(1)} %bitcast.128), channel_id=1, source_target_pairs={{0,64},{64,128},{128,192},{192,0},{1,65},{65,129},{129,193},{193,1... | collective-permute-start | bytes 786440 | tf_op jit(solution)/shard_map/ppermute | solution.py:22
  138.8 7.8 %collective-permute-start.19 = (bf16[1,1,1,8,128,128]{5,4,3,2,1,0:T(8,128)(2,1)S(1)}, bf16[1,1,1,8,128,128]{5,4,3,2,1,0:T(8,128)(2,1)S(1)}, u32[]{:S(2)}, u32[]{:S(2)}) collective-permute-start(bf16[1,1,1,8,128,128]{5,4,3,2,1,0:T(8,128)(2,1)S(1)} %bitcast.129), channel_id=1, source_target_pairs={{64,0},{128,64},{192,128},{0,192},{65,1},{129,65},{193,129},{1,193... | collective-permute-start | bytes 786440 | tf_op jit(solution)/shard_map/ppermute | solution.py:23
  141.6 5.0 %collective-permute-start.20 = (bf16[1,1,1,8,128,128]{5,4,3,2,1,0:T(8,128)(2,1)S(1)}, bf16[1,1,1,8,128,128]{5,4,3,2,1,0:T(8,128)(2,1)S(1)}, u32[]{:S(2)}, u32[]{:S(2)}) collective-permute-start(bf16[1,1,1,8,128,128]{5,4,3,2,1,0:T(8,128)(2,1)S(1)} %bitcast.130), channel_id=1, source_target_pairs={{0,8},{8,16},{16,24},{24,32},{32,40},{40,48},{48,56},{56,0},{1,9},... | collective-permute-start | bytes 786440 | tf_op jit(solution)/shard_map/ppermute | solution.py:22
  143.4 6.1 %collective-permute-start.21 = (bf16[1,1,1,8,128,128]{5,4,3,2,1,0:T(8,128)(2,1)S(1)}, bf16[1,1,1,8,128,128]{5,4,3,2,1,0:T(8,128)(2,1)S(1)}, u32[]{:S(2)}, u32[]{:S(2)}) collective-permute-start(bf16[1,1,1,8,128,128]{5,4,3,2,1,0:T(8,128)(2,1)S(1)} %bitcast.131), channel_id=1, source_target_pairs={{8,0},{16,8},{24,16},{32,24},{40,32},{48,40},{56,48},{0,56},{9,1},... | collective-permute-start | bytes 786440 | tf_op jit(solution)/shard_map/ppermute | solution.py:23
  143.8 6.6 %collective-permute-start.22 = (bf16[1,1,1,8,128,128]{5,4,3,2,1,0:T(8,128)(2,1)S(1)}, bf16[1,1,1,8,128,128]{5,4,3,2,1,0:T(8,128)(2,1)S(1)}, u32[]{:S(2)}, u32[]{:S(2)}) collective-permute-start(bf16[1,1,1,8,128,128]{5,4,3,2,1,0:T(8,128)(2,1)S(1)} %bitcast.132), channel_id=1, source_target_pairs={{0,1},{1,2},{2,3},{3,4},{4,5},{5,6},{6,7},{7,0},{8,9},{9,10},{10,1... | collective-permute-start | bytes 786440 | tf_op jit(solution)/shard_map/ppermute | solution.py:22
  146.2 5.5 %collective-permute-start.23 = (bf16[1,1,1,8,128,128]{5,4,3,2,1,0:T(8,128)(2,1)S(1)}, bf16[1,1,1,8,128,128]{5,4,3,2,1,0:T(8,128)(2,1)S(1)}, u32[]{:S(2)}, u32[]{:S(2)}) collective-permute-start(bf16[1,1,1,8,128,128]{5,4,3,2,1,0:T(8,128)(2,1)S(1)} %bitcast.133), channel_id=1, source_target_pairs={{1,0},{2,1},{3,2},{4,3},{5,4},{6,5},{7,6},{0,7},{9,8},{10,9},{11,1... | collective-permute-start | bytes 786440 | tf_op jit(solution)/shard_map/ppermute | solution.py:23
  159.4 62.7 %all-to-all-start.1 = ((bf16[64,1,128,128]{3,2,1,0:T(8,128)(2,1)}), bf16[64,1,128,128]{3,2,1,0:T(8,128)(2,1)S(1)}, u32[]{:S(2)}, u32[]{:S(2)}) async-start(bf16[64,1,128,128]{3,2,1,0:T(8,128)(2,1)} %copy.23), calls=%async_computation.1 | async-start | bytes 4194304 | tf_op jit(solution)/shard_map/all_to_all | solution.py:115
  (13 other events, 185.0 us)
where the time goes:
time: 225 us; the launch traced here: 224 us
  waiting for transfers between devices  98.5 us (44%)
  starting transfers between devices  51.2 us (23%)
  matrix products  33 us (15%)
  local copies, waits for them, and re-layouts  28.3 us (13%)
  other arithmetic  11.5 us (5%)
    all_to_all x1, waiting for transfers between devices, shards(): lax.all_to_all(outgoing_back, ('gy', 'gz'), split_axis=0, concat_axis=0,...  51.1 us
    all_to_all x1, waiting for transfers between devices, shards(): lax.all_to_all(outgoing, ('gy', 'gz'), split_axis=0, concat_axis=0, tiled...  28 us
    ppermute x12, starting transfers between devices, extended_2(): lax.ppermute(first, axis, [(b, a) for a, b in up])  19.7 us
    all_to_all x1, starting transfers between devices, shards(): lax.all_to_all(outgoing, ('gy', 'gz'), split_axis=0, concat_axis=0, tiled...  13.3 us
    ppermute x12, waiting for transfers between devices, extended_2(): lax.ppermute(last, axis, up)  11.5 us
    all_to_all x1, starting transfers between devices, shards(): lax.all_to_all(outgoing_back, ('gy', 'gz'), split_axis=0, concat_axis=0,...  10.8 us
    dot_general x1, matrix products, shards(): jnp.einsum('rij,rig->rjg', chosen_blocks, left_table, preferred_element_t...  9.37 us
    dot_general x1, matrix products, density_columns(): cube = jnp.dot(start, square, preferred_element_type=jnp.float32)  8.97 us
  transfers between devices with their start and end apart: 26, of which 14 were waited for; matrix products, arithmetic and copies ran while one was open for 22% of the time, Pallas kernels for 0%

commit v1 on v0

v1 whole, which is shorter than its diff:
```python
import functools

import jax
import jax.numpy as jnp
from jax import lax
from jax.experimental import pallas as pl
from jax.experimental.pallas import tpu as pltpu
from jax.sharding import PartitionSpec as P

B = 128
S = 6
M = 768
RMAX = 8
NOV = 4
EPSILON = 1e-06
SIDES = (("gx", 0), ("gy", 1), ("gz", 2))
F32 = jnp.float32
BF16 = jnp.bfloat16

SMEM = pl.BlockSpec(memory_space=pltpu.SMEM)
VMEM = pl.BlockSpec(memory_space=pltpu.VMEM)


def call(kernel, out_shape, ins, smem, scratch=(), limit=24, cost=None):
    return pl.pallas_call(
        kernel,
        out_shape=out_shape,
        in_specs=[SMEM] * smem + [VMEM] * (len(ins) - smem),
        out_specs=jax.tree.map(lambda _: VMEM, out_shape),
        scratch_shapes=list(scratch),
        compiler_params=pltpu.CompilerParams(vmem_limit_bytes=limit * 1024 * 1024),
        cost_estimate=cost,
    )(*ins)


def shape(dims, dtype):
    return jax.ShapeDtypeStruct(dims, dtype)


def outgoing_kernel(picks_ref, ham_ref, out_ref):
    def one(q, carry):
        out_ref[q] = ham_ref[jnp.maximum(picks_ref[q], 0)]
        return carry

    lax.fori_loop(0, out_ref.shape[0], one, 0, unroll=4)


def density_kernel(slots_ref, incoming_ref, onsite_ref, out_ref, h_ref, x_ref, q_ref):
    rows = lax.broadcasted_iota(jnp.int32, (B, B), 0)
    cols = lax.broadcasted_iota(jnp.int32, (B, B), 1)
    eye = rows == cols
    total = jnp.zeros((8, B), F32)

    def block(s, t):
        return incoming_ref[slots_ref[s * S + t]].astype(F32)

    for s in range(S):
        for t in range(s, S):
            if s == t:
                a = block(s, s)
                diag = onsite_ref[0:1, s * B : (s + 1) * B]
                h = 0.5 * (a + a.T) + jnp.where(eye, diag, 0.0)
                h_ref[s * B : (s + 1) * B, s * B : (s + 1) * B] = h
                total = total + jnp.sum((h * h).reshape(B // 8, 8, B), axis=0)
            else:
                h = 0.5 * (block(s, t) + block(t, s).T)
                h_ref[s * B : (s + 1) * B, t * B : (t + 1) * B] = h
                h_ref[t * B : (t + 1) * B, s * B : (s + 1) * B] = h.T
                total = total + 2.0 * jnp.sum((h * h).reshape(B // 8, 8, B), axis=0)
    norm = jnp.sum(jnp.sum(total, axis=0, keepdims=True), axis=1, keepdims=True)
    factor = lax.rsqrt(norm / M + EPSILON) / 1.3
    for s in range(S):
        x_ref[s * B : (s + 1) * B, :] = (h_ref[s * B : (s + 1) * B, :] * factor).astype(BF16)
    x0 = x_ref[...]
    for s in range(0, S, 2):
        part = slice(s * B, (s + 2) * B)
        q_ref[:, part] = jnp.dot(x0, x_ref[:, part], preferred_element_type=F32).astype(BF16)
    for s in range(0, S, 2):
        part = slice(s * B, (s + 2) * B)
        cube = jnp.dot(x0, q_ref[:, part], preferred_element_type=F32)
        h_ref[:, part] = 1.5 * x_ref[:, part].astype(F32) - 0.5 * cube
    x1 = h_ref[...].astype(BF16)
    column = x1[:, :B]
    inner = jnp.dot(x1, column, preferred_element_type=F32).astype(BF16)
    outer = jnp.dot(x1, inner, preferred_element_type=F32)
    for s in range(S):
        part = slice(s * B, (s + 1) * B)
        value = 1.5 * column[part].astype(F32) - 0.5 * outer[part]
        if s == 0:
            value = jnp.where(eye, 1.0, 0.0) - value
        else:
            value = 0.0 - value
        out_ref[s] = (0.5 * value).astype(BF16)


def rho_kernel(reads_ref, pick_ref, *refs):
    faces = refs[:7]
    phi_ref, rho_ref, p_ref = refs[7:]
    p_ref[...] = jnp.zeros(p_ref.shape, F32)

    def slot(r, carry):
        code = reads_ref[r]
        row = pl.multiple_of(pick_ref[r] * B, B)
        right = pick_ref[RMAX + r]
        for k in range(7):

            @pl.when((code >= k * S) & (code < (k + 1) * S))
            def _():
                at = (right, pl.ds(row, B))
                p_ref[at] = p_ref[at] + faces[k][code - k * S].astype(F32)

        return carry

    lax.fori_loop(0, RMAX, slot, 0)
    pc = jnp.concatenate([p_ref[t].astype(BF16) for t in range(NOV)], axis=1)
    width = 512
    for c in range(phi_ref.shape[1] // width):
        part = phi_ref[:, c * width : (c + 1) * width]
        mixed = jnp.dot(pc, part, preferred_element_type=F32)
        value = mixed * part.astype(F32)
        value = jnp.sum(value.reshape(NOV * B // 8, 8, width), axis=0)
        value = jnp.sum(value, axis=0, keepdims=True)
        for k in range(width // B):
            row = c * (width // B) + k
            rho_ref[row : row + 1, :] = value[:, k * B : (k + 1) * B]


def gram_kernel(pick_ref, v_ref, phi_ref, out_ref, w_ref, g_ref):
    for k in range(v_ref.shape[0]):
        part = slice(k * B, (k + 1) * B)
        w_ref[:, part] = (phi_ref[:, part].astype(F32) * v_ref[k : k + 1, :]).astype(BF16)
    for t in range(0, NOV, 2):
        g = lax.dot_general(
            phi_ref[...],
            w_ref[t * B : (t + 2) * B, :],
            (((1,), (1,)), ((), ())),
            preferred_element_type=F32,
        )
        g_ref[t] = g[:, :B]
        g_ref[t + 1] = g[:, B:]

    def slot(r, carry):
        row = pl.multiple_of(pick_ref[r] * B, B)
        out_ref[r] = g_ref[pick_ref[RMAX + r], pl.ds(row, B)].astype(BF16)
        return carry

    lax.fori_loop(0, RMAX, slot, 0)


def return_kernel(targets_ref, slots_ref, *refs):
    faces = refs[:7]
    out_ref = refs[7]

    def clear(q, carry):
        out_ref[q] = jnp.zeros((B, B), BF16)
        return carry

    lax.fori_loop(0, out_ref.shape[0], clear, 0, unroll=4)
    for k in range(7):

        def slot(r, carry):
            target = targets_ref[k * RMAX + r]

            @pl.when(target < S * S)
            def _():
                at = slots_ref[target]
                total = out_ref[at].astype(F32) + faces[k][r].astype(F32)
                out_ref[at] = total.astype(BF16)

            return carry

        lax.fori_loop(0, RMAX, slot, 0)


def owner_kernel(picks_ref, arrived_ref, out_ref):
    out_ref[...] = jnp.zeros(out_ref.shape, F32)

    def one(q, carry):
        pick = picks_ref[q]

        @pl.when(pick >= 0)
        def _():
            out_ref[pick] = out_ref[pick] + arrived_ref[q].astype(F32)

        return carry

    lax.fori_loop(0, arrived_ref.shape[0], one, 0)


def face_exchange(x):
    out = [x]
    for axis, _ in SIDES:
        size = lax.axis_size(axis)
        up = [(i, (i + 1) % size) for i in range(size)]
        out.append(lax.ppermute(x, axis, up))
        out.append(lax.ppermute(x, axis, [(b, a) for a, b in up]))
    return out


def extended(x):
    edges = {}
    for axis, dim in SIDES:
        size, length = (lax.axis_size(axis), x.shape[dim])
        up = [(i, (i + 1) % size) for i in range(size)]
        last = lax.slice_in_dim(x, length - 1, length, axis=dim)
        first = lax.slice_in_dim(x, 0, 1, axis=dim)
        edges[dim] = (
            lax.ppermute(last, axis, up),
            lax.ppermute(first, axis, [(b, a) for a, b in up]),
        )
    done = []
    for _, dim in SIDES:
        low, high = edges[dim]
        around = [(1, 1) if d in done else (0, 0) for d in range(x.ndim)]
        x = jnp.concatenate([jnp.pad(low, around), x, jnp.pad(high, around)], axis=dim)
        done.append(dim)
    return x


def jacobi_step(padded, source):
    beside_all = padded[2:, 1:-1, 1:-1] + padded[:-2, 1:-1, 1:-1]
    beside_all = beside_all + padded[1:-1, 2:, 1:-1] + padded[1:-1, :-2, 1:-1]
    beside_all = beside_all + padded[1:-1, 1:-1, 2:] + padded[1:-1, 1:-1, :-2]
    return (beside_all + source) / 6.0


def select_outgoing(picks, ham_blocks):
    return call(outgoing_kernel, shape((picks.shape[0], B, B), BF16), (picks, ham_blocks), 1)


def density_of(slots, incoming, onsite):
    return call(
        density_kernel,
        shape((S, B, B), BF16),
        (slots, incoming, onsite),
        1,
        (pltpu.VMEM((M, M), F32), pltpu.VMEM((M, M), BF16), pltpu.VMEM((M, M), BF16)),
    )


def rho_of(codes, pick, faces, tables):
    return call(
        rho_kernel,
        shape((tables.shape[1] // B, B), F32),
        (codes, pick, *faces, tables),
        2,
        (pltpu.VMEM((NOV, NOV * B, B), F32),),
    )


def gram_of(pick, potential, tables):
    return call(
        gram_kernel,
        shape((RMAX, B, B), BF16),
        (pick, potential, tables),
        1,
        (pltpu.VMEM(tables.shape, BF16), pltpu.VMEM((NOV, NOV * B, B), F32)),
    )


def returned_of(targets, slots, grams, count):
    return call(return_kernel, shape((count, B, B), BF16), (targets, slots, *grams), 2)


def owned_of(picks, arrived, held):
    return call(owner_kernel, shape((held, B, B), F32), (picks, arrived), 1)


def shards(
    ham_blocks, onsite, entry_slot, send_table, reads, gram_targets, table_pick, phi, potential_in
):
    held = ham_blocks.shape[0]
    slot_ids = entry_slot[0]
    picks = send_table.reshape(-1)
    pick = table_pick.reshape(-1)
    tables = phi.reshape(NOV * B, -1)
    outgoing = select_outgoing(picks, ham_blocks)
    incoming = lax.all_to_all(outgoing, ("gy", "gz"), split_axis=0, concat_axis=0, tiled=True)
    density = density_of(slot_ids, incoming, onsite)
    faces = face_exchange(density)
    source = rho_of(reads[0], pick, faces, tables).reshape(potential_in.shape)
    potential = potential_in
    for sweep_index in range(2):
        potential = jacobi_step(extended(potential), source)
    grams = gram_of(pick, potential.reshape(-1, B), tables)
    outgoing_back = returned_of(
        gram_targets.reshape(-1), slot_ids, face_exchange(grams), picks.shape[0]
    )
    arrived = lax.all_to_all(outgoing_back, ("gy", "gz"), split_axis=0, concat_axis=0, tiled=True)
    return (potential, owned_of(picks, arrived, held))


def solution(mesh):
    whole = ("gx", "gy", "gz")
    placed = (
        P(whole, None, None),
        P(whole, None),
        P(whole, None),
        P(whole, None, None),
        P(whole, None),
        P(whole, None, None),
        P(whole, None, None),
        P(whole, None, None, None),
        P("gx", "gy", "gz"),
    )
    return jax.shard_map(
        shards,
        mesh=mesh,
        in_specs=placed,
        out_specs=(P("gx", "gy", "gz"), P(whole, None, None)),
        check_vma=False,
    )
```

time: 225 us -> 187 us (0.83)
  matrix products: 33 us -> 0 us
  local copies, waits for them, and re-layouts: 28.3 us -> 4.17 us
  Pallas kernels: 0 us -> 19 us
  other arithmetic: 11.5 us -> 0.91 us
  waiting for transfers between devices: 98.5 us -> 109 us
    dot_general x6 -> x0, matrix products: 33 us -> none  [the longest x1 9.37 us: shards(): jnp.einsum('rij,rig->rjg', chosen_blocks, left_table, preferred_element_t...]
    pallas_call x0 -> x6, Pallas kernels: none -> 19 us  [call(): pl.pallas_call(kernel, out_shape=out_shape, in_specs=[SMEM] * smem + [VME...]
    all_to_all x1, waiting for transfers between devices: 28 us -> 46.8 us  [shards(): lax.all_to_all(outgoing, ('gy', 'gz'), split_axis=0, concat_axis=0, tiled...]
    gather x5 -> x0, local copies, waits for them, and re-layouts: 17 us -> none  [the longest x1 6.84 us: shards(): left_table = jnp.take(phi[0], table_pick[0, 0], axis=0)]
    ppermute x24, waiting for transfers between devices: 19.3 us -> 11.2 us  [the longest x6 5.68 us: face_exchange(): out.append(lax.ppermute(x, axis, [(b, a) for a, b in up]))]
    convert_element_type x1 -> x0, local copies, waits for them, and re-layouts: 3.07 us -> none  [density_columns(): wide = matrix.astype(jnp.float32)]
    reduce_sum x1 -> x0, other arithmetic: 3.05 us -> none  [density_columns(): factor = lax.rsqrt(jnp.sum(hamilton * hamilton) / M + EPSILON) / 1.3]
    reshape x1 -> x2, local copies, waits for them, and re-layouts: 2.7 us -> 0.16 us  [the longest x1 0.08 us: shards(): pick = table_pick.reshape(-1)]
  transfers between devices with their start and end apart: 26 -> 26, of which waited for: 14 -> 10; matrix products, arithmetic and copies ran while one was open for 22% -> 1% of each run, Pallas kernels for 0% -> 4%
where the time goes in v1:
time: 187 us
  waiting for transfers between devices  109 us (58%)
  starting transfers between devices  53 us (28%)
  Pallas kernels  19 us (10%)
  local copies, waits for them, and re-layouts  4.17 us (2%)
    all_to_all x1, waiting for transfers between devices, shards(): lax.all_to_all(outgoing_back, ('gy', 'gz'), split_axis=0, concat_axis=0,...  51.1 us
    all_to_all x1, waiting for transfers between devices, shards(): lax.all_to_all(outgoing, ('gy', 'gz'), split_axis=0, concat_axis=0, tiled...  46.8 us
    pallas_call x6, Pallas kernels, call(): pl.pallas_call(kernel, out_shape=out_shape, in_specs=[SMEM] * smem + [VME...  19 us
    all_to_all x1, starting transfers between devices, shards(): lax.all_to_all(outgoing, ('gy', 'gz'), split_axis=0, concat_axis=0, tiled...  13.3 us
    all_to_all x1, starting transfers between devices, shards(): lax.all_to_all(outgoing_back, ('gy', 'gz'), split_axis=0, concat_axis=0,...  12.8 us
    ppermute x6, starting transfers between devices, extended(): lax.ppermute(first, axis, [(b, a) for a, b in up])  9.06 us
    ppermute x6, starting transfers between devices, face_exchange(): out.append(lax.ppermute(x, axis, [(b, a) for a, b in up]))  6.84 us
    ppermute x6, starting transfers between devices, face_exchange(): out.append(lax.ppermute(x, axis, up))  6.51 us
  transfers between devices with their start and end apart: 26, of which 10 were waited for; matrix products, arithmetic and copies ran while one was open for 1% of the time, Pallas kernels for 4%

profile of v1, /device:TPU:1, one launch (start us, length us, event | category | flops | bytes accessed | tf_op | source)
XLA Modules:
  0.0 187.0 jit_solution(17183284886264713213)
XLA Ops:
  2.2 2.1 %shard_map.104 = bf16[64,128,128]{2,1,0:T(8,128)(2,1)} custom-call(s32[64]{0:T(128)S(1)} %bitcast.15, bf16[8,128,128]{2,1,0:T(8,128)(2,1)S(1)} %copy-done.2), custom_call_target="tpu_custom_call" | custom-call | tf_op jit(solution)/shard_map/pallas_call | solution.py:25
  4.4 13.3 %all-to-all-start = ((bf16[64,128,128]{2,1,0:T(8,128)(2,1)}), bf16[64,128,128]{2,1,0:T(8,128)(2,1)S(1)}, u32[]{:S(2)}, u32[]{:S(2)}) async-start(bf16[64,128,128]{2,1,0:T(8,128)(2,1)} %shard_map.104), calls=%async_computation | async-start | bytes 4194304 | tf_op jit(solution)/shard_map/all_to_all | solution.py:278
  19.4 1.5 collective-permute-start
  20.9 1.9 collective-permute-start.3
  22.7 46.8 %all-to-all-done.incoming_ref = bf16[64,128,128]{2,1,0:T(8,128)(2,1)S(1)} async-done(((bf16[64,128,128]{2,1,0:T(8,128)(2,1)}), bf16[64,128,128]{2,1,0:T(8,128)(2,1)S(1)}, u32[]{:S(2)}, u32[]{:S(2)}) %all-to-all-start) | async-done | bytes 2097184 | tf_op jit(solution)/shard_map/all_to_all | solution.py:278
  69.5 4.4 %shard_map.105.refs_0_ = bf16[6,128,128]{2,1,0:T(8,128)(2,1)S(1)} custom-call(s32[36]{0:T(128)S(1)} %bitcast.13, bf16[64,128,128]{2,1,0:T(8,128)(2,1)S(1)} %all-to-all-done.incoming_ref, f32[1,768]{1,0:T(1,128)S(1)} %copy-done.3), custom_call_target="tpu_custom_call" | custom-call | tf_op jit(solution)/shard_map/pallas_call | solution.py:25
  75.4 1.5 collective-permute-start.7
  77.6 2.3 %collective-permute-start.10 = (bf16[6,128,128]{2,1,0:T(8,128)(2,1)S(1)}, bf16[6,128,128]{2,1,0:T(8,128)(2,1)S(1)}, u32[]{:S(2)}, u32[]{:S(2)}) collective-permute-start(bf16[6,128,128]{2,1,0:T(8,128)(2,1)S(1)} %shard_map.105.refs_0_), channel_id=1, source_target_pairs={{0,1},{1,2},{2,3},{3,4},{4,5},{5,6},{6,7},{7,0},{8,9},{9,10},{10,1... | collective-permute-start | bytes 589832 | tf_op jit(solution)/shard_map/ppermute | solution.py:195
  79.8 1.6 collective-permute-done.6.refs_1_
  83.0 1.7 collective-permute-start.4
  84.7 2.8 %collective-permute-done.11.refs_6_ = bf16[6,128,128]{2,1,0:T(8,128)(2,1)S(1)} collective-permute-done((bf16[6,128,128]{2,1,0:T(8,128)(2,1)S(1)}, bf16[6,128,128]{2,1,0:T(8,128)(2,1)S(1)}, u32[]{:S(2)}, u32[]{:S(2)}) %collective-permute-start.11) | collective-permute-done | bytes 196640 | tf_op jit(solution)/shard_map/ppermute | solution.py:196
  87.5 2.2 %copy-done = bf16[1,4,128,4096]{3,2,1,0:T(8,128)(2,1)S(1)} copy-done((bf16[1,4,128,4096]{3,2,1,0:T(8,128)(2,1)S(1)}, bf16[1,4,128,4096]{3,2,1,0:T(8,128)(2,1)}, u32[]{:S(2)}) %copy-start) | copy-done | bytes 4194328
  89.7 3.4 %shard_map.106 = f32[32,128]{1,0:T(8,128)S(1)} custom-call(s32[8]{0:T(128)S(1)} %bitcast.17, s32[16]{0:T(128)S(1)} %reshape.22.pick_ref, bf16[6,128,128]{2,1,0:T(8,128)(2,1)S(1)} %shard_map.105.refs_0_, bf16[6,128,128]{2,1,0:T(8,128)(2,1)S(1)} %collective-permute-done.6.refs_1_, bf16[6,128,128]{2,1,0:T(8,128)(2,1)S(1)} %collective-permute-done.7.refs_2_, ...), custom_call_target="tpu_custom_call" | custom-call | tf_op jit(solution)/shard_map/pallas_call | solution.py:25
  93.2 1.5 collective-permute-start.14
  96.5 2.7 %collective-permute-start.16 = (f32[4,8,1]{2,1,0:T(8,128)S(1)}, f32[4,8,1]{2,1,0:T(8,128)S(1)}, u32[]{:S(2)}, u32[]{:S(2)}) collective-permute-start(f32[4,8,1]{2,1,0:T(8,128)S(1)} %get-tuple-element.2), channel_id=1, source_target_pairs={{1,0},{2,1},{3,2},{4,3},{5,4},{6,5},{7,6},{0,7},{9,8},{10,9},{11,1... | collective-permute-start | bytes 392 | tf_op jit(solution)/shard_map/ppermute | solution.py:209
  100.5 3.2 %shard_map.107.refs_0_ = bf16[8,128,128]{2,1,0:T(8,128)(2,1)S(1)} custom-call(s32[16]{0:T(128)S(1)} %reshape.22.pick_ref, f32[32,128]{1,0:T(8,128)S(1)} %fusion.24.v_ref, bf16[512,4096]{1,0:T(8,128)(2,1)S(1)} %bitcast.12), custom_call_target="tpu_custom_call" | custom-call | tf_op jit(solution)/shard_map/pallas_call | solution.py:25
  103.8 2.7 %collective-permute-start.19 = (bf16[8,128,128]{2,1,0:T(8,128)(2,1)S(1)}, bf16[8,128,128]{2,1,0:T(8,128)(2,1)S(1)}, u32[]{:S(2)}, u32[]{:S(2)}) collective-permute-start(bf16[8,128,128]{2,1,0:T(8,128)(2,1)S(1)} %shard_map.107.refs_0_), channel_id=1, source_target_pairs={{64,0},{128,64},{192,128},{0,192},{65,1},{129,65},{193,129},{1,193... | collective-permute-start | bytes 786440 | tf_op jit(solution)/shard_map/ppermute | solution.py:196
  106.5 2.3 %collective-permute-start.20 = (bf16[8,128,128]{2,1,0:T(8,128)(2,1)S(1)}, bf16[8,128,128]{2,1,0:T(8,128)(2,1)S(1)}, u32[]{:S(2)}, u32[]{:S(2)}) collective-permute-start(bf16[8,128,128]{2,1,0:T(8,128)(2,1)S(1)} %shard_map.107.refs_0_), channel_id=1, source_target_pairs={{0,8},{8,16},{16,24},{24,32},{32,40},{40,48},{48,56},{56,0},{1,9},... | collective-permute-start | bytes 786440 | tf_op jit(solution)/shard_map/ppermute | solution.py:195
  109.0 1.9 %collective-permute-done.18.refs_1_ = bf16[8,128,128]{2,1,0:T(8,128)(2,1)S(1)} collective-permute-done((bf16[8,128,128]{2,1,0:T(8,128)(2,1)S(1)}, bf16[8,128,128]{2,1,0:T(8,128)(2,1)S(1)}, u32[]{:S(2)}, u32[]{:S(2)}) %collective-permute-start.18) | collective-permute-done | bytes 262176 | tf_op jit(solution)/shard_map/ppermute | solution.py:195
  110.9 2.4 %collective-permute-start.23 = (bf16[8,128,128]{2,1,0:T(8,128)(2,1)S(1)}, bf16[8,128,128]{2,1,0:T(8,128)(2,1)S(1)}, u32[]{:S(2)}, u32[]{:S(2)}) collective-permute-start(bf16[8,128,128]{2,1,0:T(8,128)(2,1)S(1)} %shard_map.107.refs_0_), channel_id=1, source_target_pairs={{1,0},{2,1},{3,2},{4,3},{5,4},{6,5},{7,6},{0,7},{9,8},{10,9},{11,1... | collective-permute-start | bytes 786440 | tf_op jit(solution)/shard_map/ppermute | solution.py:196
  116.6 3.3 %shard_map.108 = bf16[64,128,128]{2,1,0:T(8,128)(2,1)} custom-call(s32[56]{0:T(128)S(1)} %reshape.26.targets_ref, s32[36]{0:T(128)S(1)} %bitcast.14, bf16[8,128,128]{2,1,0:T(8,128)(2,1)S(1)} %shard_map.107.refs_0_, bf16[8,128,128]{2,1,0:T(8,128)(2,1)S(1)} %collective-permute-done.18.refs_1_, bf16[8,128,128]{2,1,0:T(8,128)(2,1)S(1)} %collective-permute-done.19.refs_2_, ...), custom_call_target="tpu_custom_call" | custom-call | tf_op jit(solution)/shard_map/pallas_call | solution.py:25
  120.0 12.8 %all-to-all-start.1 = ((bf16[64,128,128]{2,1,0:T(8,128)(2,1)}), bf16[64,128,128]{2,1,0:T(8,128)(2,1)S(1)}, u32[]{:S(2)}, u32[]{:S(2)}) async-start(bf16[64,128,128]{2,1,0:T(8,128)(2,1)} %shard_map.108), calls=%async_computation.1 | async-start | bytes 4194304 | tf_op jit(solution)/shard_map/all_to_all | solution.py:289
  133.4 51.1 %all-to-all-done.1.arrived_ref = bf16[64,128,128]{2,1,0:T(8,128)(2,1)S(1)} async-done(((bf16[64,128,128]{2,1,0:T(8,128)(2,1)}), bf16[64,128,128]{2,1,0:T(8,128)(2,1)S(1)}, u32[]{:S(2)}, u32[]{:S(2)}) %all-to-all-start.1) | async-done | bytes 2097184 | tf_op jit(solution)/shard_map/all_to_all | solution.py:289
  184.6 2.4 %shard_map.109 = f32[8,128,128]{2,1,0:T(8,128)} custom-call(s32[64]{0:T(128)S(1)} %bitcast.16, bf16[64,128,128]{2,1,0:T(8,128)(2,1)S(1)} %all-to-all-done.1.arrived_ref), custom_call_target="tpu_custom_call" | custom-call | tf_op jit(solution)/shard_map/pallas_call | solution.py:25
  (75 shorter events, 14.4 us)
Async XLA Ops:
  4.4 65.1 %all-to-all-start = ((bf16[64,128,128]{2,1,0:T(8,128)(2,1)}), bf16[64,128,128]{2,1,0:T(8,128)(2,1)S(1)}, u32[]{:S(2)}, u32[]{:S(2)}) async-start(bf16[64,128,128]{2,1,0:T(8,128)(2,1)} %shard_map.104), calls=%async_computation | async-start | bytes 4194304 | tf_op jit(solution)/shard_map/all_to_all | solution.py:278
  17.7 57.6 %collective-permute-start.2 = (f32[4,1,128]{2,1,0:T(1,128)S(1)}, f32[4,1,128]{2,1,0:T(1,128)S(1)}, u32[]{:S(2)}, u32[]{:S(2)}) collective-permute-start(f32[4,1,128]{2,1,0:T(1,128)S(1)} %get-tuple-element.11), channel_id=1, source_target_pairs={{8,0},{16,8},{24,16},{32,24},{40,32},{48,40},{56,48},{0,56},{9,1},... | collective-permute-start | bytes 6152 | tf_op jit(solution)/shard_map/ppermute | solution.py:209
  18.2 57.2 %collective-permute-start.1 = (f32[1,8,128]{2,1,0:T(8,128)S(1)}, f32[1,8,128]{2,1,0:T(8,128)S(1)}, u32[]{:S(2)}, u32[]{:S(2)}) collective-permute-start(f32[1,8,128]{2,1,0:T(8,128)S(1)} %get-tuple-element.13), channel_id=1, source_target_pairs={{0,64},{64,128},{128,192},{192,0},{1,65},{65,129},{129,193},{193,1... | collective-permute-start | bytes 12296 | tf_op jit(solution)/shard_map/ppermute | solution.py:208
  19.4 58.2 %collective-permute-start = (f32[1,8,128]{2,1,0:T(8,128)S(1)}, f32[1,8,128]{2,1,0:T(8,128)S(1)}, u32[]{:S(2)}, u32[]{:S(2)}) collective-permute-start(f32[1,8,128]{2,1,0:T(8,128)S(1)} %get-tuple-element.12), channel_id=1, source_target_pairs={{64,0},{128,64},{192,128},{0,192},{65,1},{129,65},{193,129},{1,193... | collective-permute-start | bytes 12296 | tf_op jit(solution)/shard_map/ppermute | solution.py:209
  20.9 54.5 %collective-permute-start.3 = (f32[4,1,128]{2,1,0:T(1,128)S(1)}, f32[4,1,128]{2,1,0:T(1,128)S(1)}, u32[]{:S(2)}, u32[]{:S(2)}) collective-permute-start(f32[4,1,128]{2,1,0:T(1,128)S(1)} %get-tuple-element.10), channel_id=1, source_target_pairs={{0,8},{8,16},{16,24},{24,32},{32,40},{40,48},{48,56},{56,0},{1,9},... | collective-permute-start | bytes 6152 | tf_op jit(solution)/shard_map/ppermute | solution.py:208
  73.9 7.5 %collective-permute-start.6 = (bf16[6,128,128]{2,1,0:T(8,128)(2,1)S(1)}, bf16[6,128,128]{2,1,0:T(8,128)(2,1)S(1)}, u32[]{:S(2)}, u32[]{:S(2)}) collective-permute-start(bf16[6,128,128]{2,1,0:T(8,128)(2,1)S(1)} %shard_map.105.refs_0_), channel_id=1, source_target_pairs={{0,64},{64,128},{128,192},{192,0},{1,65},{65,129},{129,193},{193,1... | collective-permute-start | bytes 589832 | tf_op jit(solution)/shard_map/ppermute | solution.py:195
  75.4 6.6 %collective-permute-start.7 = (bf16[6,128,128]{2,1,0:T(8,128)(2,1)S(1)}, bf16[6,128,128]{2,1,0:T(8,128)(2,1)S(1)}, u32[]{:S(2)}, u32[]{:S(2)}) collective-permute-start(bf16[6,128,128]{2,1,0:T(8,128)(2,1)S(1)} %shard_map.105.refs_0_), channel_id=1, source_target_pairs={{64,0},{128,64},{192,128},{0,192},{65,1},{129,65},{193,129},{1,193... | collective-permute-start | bytes 589832 | tf_op jit(solution)/shard_map/ppermute | solution.py:196
  77.0 6.0 %collective-permute-start.8 = (bf16[6,128,128]{2,1,0:T(8,128)(2,1)S(1)}, bf16[6,128,128]{2,1,0:T(8,128)(2,1)S(1)}, u32[]{:S(2)}, u32[]{:S(2)}) collective-permute-start(bf16[6,128,128]{2,1,0:T(8,128)(2,1)S(1)} %shard_map.105.refs_0_), channel_id=1, source_target_pairs={{0,8},{8,16},{16,24},{24,32},{32,40},{40,48},{48,56},{56,0},{1,9},... | collective-permute-start | bytes 589832 | tf_op jit(solution)/shard_map/ppermute | solution.py:195
  77.6 7.1 %collective-permute-start.9 = (bf16[6,128,128]{2,1,0:T(8,128)(2,1)S(1)}, bf16[6,128,128]{2,1,0:T(8,128)(2,1)S(1)}, u32[]{:S(2)}, u32[]{:S(2)}) collective-permute-start(bf16[6,128,128]{2,1,0:T(8,128)(2,1)S(1)} %shard_map.105.refs_0_), channel_id=1, source_target_pairs={{8,0},{16,8},{24,16},{32,24},{40,32},{48,40},{56,48},{0,56},{9,1},... | collective-permute-start | bytes 589832 | tf_op jit(solution)/shard_map/ppermute | solution.py:196
  77.6 7.1 %collective-permute-start.10 = (bf16[6,128,128]{2,1,0:T(8,128)(2,1)S(1)}, bf16[6,128,128]{2,1,0:T(8,128)(2,1)S(1)}, u32[]{:S(2)}, u32[]{:S(2)}) collective-permute-start(bf16[6,128,128]{2,1,0:T(8,128)(2,1)S(1)} %shard_map.105.refs_0_), channel_id=1, source_target_pairs={{0,1},{1,2},{2,3},{3,4},{4,5},{5,6},{6,7},{7,0},{8,9},{9,10},{10,1... | collective-permute-start | bytes 589832 | tf_op jit(solution)/shard_map/ppermute | solution.py:195
  81.4 6.0 %collective-permute-start.11 = (bf16[6,128,128]{2,1,0:T(8,128)(2,1)S(1)}, bf16[6,128,128]{2,1,0:T(8,128)(2,1)S(1)}, u32[]{:S(2)}, u32[]{:S(2)}) collective-permute-start(bf16[6,128,128]{2,1,0:T(8,128)(2,1)S(1)} %shard_map.105.refs_0_), channel_id=1, source_target_pairs={{1,0},{2,1},{3,2},{4,3},{5,4},{6,5},{7,6},{0,7},{9,8},{10,9},{11,1... | collective-permute-start | bytes 589832 | tf_op jit(solution)/shard_map/ppermute | solution.py:196
  82.0 11.1 %collective-permute-start.5 = (f32[4,8,1]{2,1,0:T(8,128)S(1)}, f32[4,8,1]{2,1,0:T(8,128)S(1)}, u32[]{:S(2)}, u32[]{:S(2)}) collective-permute-start(f32[4,8,1]{2,1,0:T(8,128)S(1)} %get-tuple-element.9), channel_id=1, source_target_pairs={{0,1},{1,2},{2,3},{3,4},{4,5},{5,6},{6,7},{7,0},{8,9},{9,10},{10,1... | collective-permute-start | bytes 392 | tf_op jit(solution)/shard_map/ppermute | solution.py:208
  83.0 10.1 %collective-permute-start.4 = (f32[4,8,1]{2,1,0:T(8,128)S(1)}, f32[4,8,1]{2,1,0:T(8,128)S(1)}, u32[]{:S(2)}, u32[]{:S(2)}) collective-permute-start(f32[4,8,1]{2,1,0:T(8,128)S(1)} %get-tuple-element.8), channel_id=1, source_target_pairs={{1,0},{2,1},{3,2},{4,3},{5,4},{6,5},{7,6},{0,7},{9,8},{10,9},{11,1... | collective-permute-start | bytes 392 | tf_op jit(solution)/shard_map/ppermute | solution.py:209
  94.7 4.5 %collective-permute-start.15 = (f32[4,1,128]{2,1,0:T(1,128)S(1)}, f32[4,1,128]{2,1,0:T(1,128)S(1)}, u32[]{:S(2)}, u32[]{:S(2)}) collective-permute-start(f32[4,1,128]{2,1,0:T(1,128)S(1)} %get-tuple-element.6), channel_id=1, source_target_pairs={{0,8},{8,16},{16,24},{24,32},{32,40},{40,48},{48,56},{56,0},{1,9},... | collective-permute-start | bytes 6152 | tf_op jit(solution)/shard_map/ppermute | solution.py:208
  95.0 5.3 %collective-permute-start.12 = (f32[1,8,128]{2,1,0:T(8,128)S(1)}, f32[1,8,128]{2,1,0:T(8,128)S(1)}, u32[]{:S(2)}, u32[]{:S(2)}) collective-permute-start(f32[1,8,128]{2,1,0:T(8,128)S(1)} %get-tuple-element.5), channel_id=1, source_target_pairs={{64,0},{128,64},{192,128},{0,192},{65,1},{129,65},{193,129},{1,193... | collective-permute-start | bytes 12296 | tf_op jit(solution)/shard_map/ppermute | solution.py:209
  96.3 4.1 %collective-permute-start.13 = (f32[1,8,128]{2,1,0:T(8,128)S(1)}, f32[1,8,128]{2,1,0:T(8,128)S(1)}, u32[]{:S(2)}, u32[]{:S(2)}) collective-permute-start(f32[1,8,128]{2,1,0:T(8,128)S(1)} %get-tuple-element.4), channel_id=1, source_target_pairs={{0,64},{64,128},{128,192},{192,0},{1,65},{65,129},{129,193},{193,1... | collective-permute-start | bytes 12296 | tf_op jit(solution)/shard_map/ppermute | solution.py:208
  96.5 3.8 %collective-permute-start.17 = (f32[4,8,1]{2,1,0:T(8,128)S(1)}, f32[4,8,1]{2,1,0:T(8,128)S(1)}, u32[]{:S(2)}, u32[]{:S(2)}) collective-permute-start(f32[4,8,1]{2,1,0:T(8,128)S(1)} %get-tuple-element.3), channel_id=1, source_target_pairs={{0,1},{1,2},{2,3},{3,4},{4,5},{5,6},{6,7},{7,0},{8,9},{9,10},{10,1... | collective-permute-start | bytes 392 | tf_op jit(solution)/shard_map/ppermute | solution.py:208
  103.7 7.2 %collective-permute-start.18 = (bf16[8,128,128]{2,1,0:T(8,128)(2,1)S(1)}, bf16[8,128,128]{2,1,0:T(8,128)(2,1)S(1)}, u32[]{:S(2)}, u32[]{:S(2)}) collective-permute-start(bf16[8,128,128]{2,1,0:T(8,128)(2,1)S(1)} %shard_map.107.refs_0_), channel_id=1, source_target_pairs={{0,64},{64,128},{128,192},{192,0},{1,65},{65,129},{129,193},{193,1... | collective-permute-start | bytes 786440 | tf_op jit(solution)/shard_map/ppermute | solution.py:195
  103.8 9.6 %collective-permute-start.19 = (bf16[8,128,128]{2,1,0:T(8,128)(2,1)S(1)}, bf16[8,128,128]{2,1,0:T(8,128)(2,1)S(1)}, u32[]{:S(2)}, u32[]{:S(2)}) collective-permute-start(bf16[8,128,128]{2,1,0:T(8,128)(2,1)S(1)} %shard_map.107.refs_0_), channel_id=1, source_target_pairs={{64,0},{128,64},{192,128},{0,192},{65,1},{129,65},{193,129},{1,193... | collective-permute-start | bytes 786440 | tf_op jit(solution)/shard_map/ppermute | solution.py:196
  106.5 7.0 %collective-permute-start.20 = (bf16[8,128,128]{2,1,0:T(8,128)(2,1)S(1)}, bf16[8,128,128]{2,1,0:T(8,128)(2,1)S(1)}, u32[]{:S(2)}, u32[]{:S(2)}) collective-permute-start(bf16[8,128,128]{2,1,0:T(8,128)(2,1)S(1)} %shard_map.107.refs_0_), channel_id=1, source_target_pairs={{0,8},{8,16},{16,24},{24,32},{32,40},{40,48},{48,56},{56,0},{1,9},... | collective-permute-start | bytes 786440 | tf_op jit(solution)/shard_map/ppermute | solution.py:195
  108.7 6.1 %collective-permute-start.21 = (bf16[8,128,128]{2,1,0:T(8,128)(2,1)S(1)}, bf16[8,128,128]{2,1,0:T(8,128)(2,1)S(1)}, u32[]{:S(2)}, u32[]{:S(2)}) collective-permute-start(bf16[8,128,128]{2,1,0:T(8,128)(2,1)S(1)} %shard_map.107.refs_0_), channel_id=1, source_target_pairs={{8,0},{16,8},{24,16},{32,24},{40,32},{48,40},{56,48},{0,56},{9,1},... | collective-permute-start | bytes 786440 | tf_op jit(solution)/shard_map/ppermute | solution.py:196
  109.0 6.7 %collective-permute-start.22 = (bf16[8,128,128]{2,1,0:T(8,128)(2,1)S(1)}, bf16[8,128,128]{2,1,0:T(8,128)(2,1)S(1)}, u32[]{:S(2)}, u32[]{:S(2)}) collective-permute-start(bf16[8,128,128]{2,1,0:T(8,128)(2,1)S(1)} %shard_map.107.refs_0_), channel_id=1, source_target_pairs={{0,1},{1,2},{2,3},{3,4},{4,5},{5,6},{6,7},{7,0},{8,9},{9,10},{10,1... | collective-permute-start | bytes 786440 | tf_op jit(solution)/shard_map/ppermute | solution.py:195
  110.9 5.7 %collective-permute-start.23 = (bf16[8,128,128]{2,1,0:T(8,128)(2,1)S(1)}, bf16[8,128,128]{2,1,0:T(8,128)(2,1)S(1)}, u32[]{:S(2)}, u32[]{:S(2)}) collective-permute-start(bf16[8,128,128]{2,1,0:T(8,128)(2,1)S(1)} %shard_map.107.refs_0_), channel_id=1, source_target_pairs={{1,0},{2,1},{3,2},{4,3},{5,4},{6,5},{7,6},{0,7},{9,8},{10,9},{11,1... | collective-permute-start | bytes 786440 | tf_op jit(solution)/shard_map/ppermute | solution.py:196
  120.0 64.6 %all-to-all-start.1 = ((bf16[64,128,128]{2,1,0:T(8,128)(2,1)}), bf16[64,128,128]{2,1,0:T(8,128)(2,1)S(1)}, u32[]{:S(2)}, u32[]{:S(2)}) async-start(bf16[64,128,128]{2,1,0:T(8,128)(2,1)} %shard_map.108), calls=%async_computation.1 | async-start | bytes 4194304 | tf_op jit(solution)/shard_map/all_to_all | solution.py:289
  (13 other events, 370.0 us)
